TPU v7x, 32 devices: a whole 2x2x4 slice. The times are simulated.
32 devices in a mesh: head: 4 (over z), pts: 8 (over y, x, core).
Axes of the slice: x: 2, y: 2, z: 4, core: 2. Of those that a mesh axis runs over, the one named last changes fastest.
Arguments:
- layer_inputs_trainorder: bfloat16 [196608, 256], P(('head', 'pts')), may hold values from -6 to 6
- inference_placement: int32 [196608], P(('head', 'pts')), may hold values from 0 to 196607, as said below
- initial_layernorm_gain: float32 [256], replicated, may hold values from 0.1 to 1.9
- initial_layernorm_offset: float32 [256], replicated, may hold values from -2 to 2
- attribute_projection: bfloat16 [256, 256], replicated, may hold values from -0.375 to 0.375
- assignment_feeder_projection: bfloat16 [256, 256], replicated, may hold values from -0.375 to 0.375
- partition_projection: bfloat16 [16, 32], replicated, may hold values from -1.5 to 1.5
- partition_offset: float32 [32], replicated, may hold values from -4 to 4
- softmax_sharpness: float32 [16], P('head'), may hold values from 0.03 to 1
- partition_question_map: float32 [16, 16], replicated, may hold values from -1.5 to 1.5
- partition_lookup_map: float32 [16, 16], replicated, may hold values from -1.5 to 1.5
- partition_content_map: float32 [16, 16], replicated, may hold values from -1.5 to 1.5
- emitted_projection: bfloat16 [256, 256], replicated, may hold values from -0.375 to 0.375
- emitted_offset: float32 [256], replicated, may hold values from -2 to 2
- latter_layernorm_gain: float32 [256], replicated, may hold values from 0.1 to 1.9
- latter_layernorm_offset: float32 [256], replicated, may hold values from -2 to 2
- perceptron_entry_map: bfloat16 [256, 1024], replicated, may hold values from -0.375 to 0.375
- perceptron_entry_offset: float32 [1024], replicated, may hold values from -2 to 2
- perceptron_exit_map: bfloat16 [1024, 256], replicated, may hold values from -0.1875 to 0.1875
- perceptron_exit_offset: float32 [256], replicated, may hold values from -2 to 2
Outputs:
- served: bfloat16 [8, 24576, 256], P('pts', 'head')
Inputs may be any that keep to these rules, and one draw needn't show every extreme that they name: inference_placement is a permutation of all points; of the 6144 points of each aligned block of the training order, exactly 192 go to each aligned block of 6144 serving positions.
All inputs are finite; a program needn't handle non-finite values.
Results may differ from a plain program's by a relative error of at most 0.0035.
The roundings to bfloat16 on the way count: a program that leaves them out, or rounds other values in their place, can miss the bound.
Values may be sent and summed in bfloat16 or wider, within the bound.
A program may use at most 128 MiB of HBM per device.

v0:
```python
import functools
import math

import jax
import jax.numpy as jnp
from jax import lax
from jax.experimental import pallas as pl
from jax.experimental.pallas import tpu as pltpu
from jax.sharding import PartitionSpec as P

DH = 16
TILE = 512
SHARES = (5, 4, 3)
F32 = jnp.float32
BF16 = jnp.bfloat16
HIGHEST = lax.Precision.HIGHEST
LOG2E = math.log2(math.e)
NT = (((1,), (1,)), ((), ()))


def norm_rows(rows, gain, bias):
    mean = jnp.mean(rows, axis=-1, keepdims=True)
    centred = rows - mean
    spread = jnp.mean(centred * centred, axis=-1, keepdims=True)
    return (centred * lax.rsqrt(spread + 1e-05) * gain + bias).astype(BF16)


def slice_weights(feeder_t, expand, offset, scale, slices):
    raw = jnp.dot(expand, feeder_t, preferred_element_type=F32)
    logit = (raw + offset) * scale
    lanes = logit.shape[1]
    logit = logit.reshape(-1, slices, lanes)
    powers = jnp.exp2(logit - jnp.max(logit, axis=1, keepdims=True))
    share = powers * (1.0 / jnp.sum(powers, axis=1, keepdims=True))
    return share.reshape(-1, lanes)


def same_head(shape, row_size, column_size):
    row_head = lax.broadcasted_iota(jnp.int32, shape, 0) // row_size
    column_head = lax.broadcasted_iota(jnp.int32, shape, 1) // column_size
    return row_head == column_head


def sums_kernel(
    slices, x_ref, gain_ref, bias_ref, attribute_ref, feeder_ref, project_ref, offset_row_ref,
    sharp_row_ref, out_ref, w_ref, expand_ref, offset_ref, scale_ref, numer, total,
):
    step = pl.program_id(0)
    width = x_ref.shape[1]

    @pl.when(step == 0)
    def _():
        numer[...] = jnp.zeros_like(numer)
        total[...] = jnp.zeros_like(total)
        w_ref[:width] = attribute_ref[...].astype(F32).T.astype(BF16)
        w_ref[width:] = feeder_ref[...].astype(F32).T.astype(BF16)
        columns, heads = offset_ref.shape[0], sharp_row_ref.shape[1]
        stacked = jnp.concatenate([project_ref[...].astype(F32).T] * heads, axis=0)
        lane = lax.broadcasted_iota(jnp.int32, (DH, width), 1) % DH
        pick = (lane == lax.broadcasted_iota(jnp.int32, (DH, width), 0)).astype(BF16)
        filled = jnp.dot(stacked.astype(BF16), pick, preferred_element_type=F32)
        expand_ref[...] = jnp.where(
            same_head(filled.shape, slices, DH), filled, 0.0
        ).astype(BF16)
        own = same_head((columns, heads), slices, 1)
        sharp = jnp.sum(jnp.where(own, sharp_row_ref[...], 0.0), axis=1, keepdims=True)
        scale_ref[...] = LOG2E / sharp
        row = lax.broadcasted_iota(jnp.int32, (columns, slices), 0) % slices
        match = row == lax.broadcasted_iota(jnp.int32, (columns, slices), 1)
        offset_ref[...] = jnp.sum(
            jnp.where(match, offset_row_ref[...], 0.0), axis=1, keepdims=True
        )

    normed = norm_rows(x_ref[...].astype(F32), gain_ref[...], bias_ref[...])
    both = lax.dot_general(w_ref[...], normed, NT, preferred_element_type=F32).astype(BF16)
    share = slice_weights(
        both[width:], expand_ref[...], offset_ref[...], scale_ref[...], slices
    )
    numer[...] += lax.dot_general(
        both[:width], share.astype(BF16), NT, preferred_element_type=F32
    )
    lanes = total.shape[1]
    part = share[:, :lanes]
    for at in range(lanes, share.shape[1], lanes):
        part += share[:, at : at + lanes]
    total[...] += part

    @pl.when(step == pl.num_programs(0) - 1)
    def _():
        kept = jnp.where(same_head(numer.shape, DH, slices), numer[...], 0.0)
        out_ref[:DH] = jnp.sum(kept.reshape(-1, DH, kept.shape[1]), axis=0)
        out_ref[DH:] = lax.dot_general(
            jnp.ones((8, lanes), F32), total[...], NT, precision=HIGHEST,
            preferred_element_type=F32,
        )


def exact_gelu(h):
    half = 0.5 * h
    return half + half * lax.erf(h * (1.0 / math.sqrt(2.0)))


def blend_kernel(slices, sums_ref, question_ref, lookup_ref, content_ref, blend):
    stok = sums_ref[:DH] / (sums_ref[DH : DH + 1] + 1e-05)
    query, key, value = (
        jnp.dot(m[...].T, stok, precision=HIGHEST, preferred_element_type=F32)
        for m in (question_ref, lookup_ref, content_ref)
    )
    scores = jnp.dot(key.T, query, precision=HIGHEST, preferred_element_type=F32)
    scores = scores * (1.0 / math.sqrt(DH))
    mask = same_head(scores.shape, slices, slices)
    scores = jnp.where(mask, scores, -jnp.inf)
    powers = jnp.exp(scores - jnp.max(scores, axis=0, keepdims=True))
    attention = powers / jnp.sum(powers, axis=0, keepdims=True)
    sout = jnp.dot(value, attention, precision=HIGHEST, preferred_element_type=F32)
    spread = jnp.concatenate([sout] * (blend.shape[0] // DH), axis=0)
    blend[...] = jnp.where(same_head(blend.shape, DH, slices), spread, 0.0).astype(BF16)


def rows_kernel(
    slices, x_ref, blend, gain_ref, bias_ref, w_ref, expand_ref, offset_ref,
    scale_ref, emit_ref, emit_bias_ref, gain2_ref, bias2_ref, entry_ref, entry_bias_ref,
    exit_ref, exit_bias_ref, *earlier_and_out,
):
    out_ref = earlier_and_out[-1]
    width = x_ref.shape[1]
    x = x_ref[...].astype(F32)
    normed = norm_rows(x, gain_ref[...], bias_ref[...])
    feeder = lax.dot_general(w_ref[width:], normed, NT, preferred_element_type=F32).astype(BF16)
    share = slice_weights(feeder, expand_ref[...], offset_ref[...], scale_ref[...], slices)
    mixed = jnp.dot(blend[...], share.astype(BF16), preferred_element_type=F32)
    y = (
        x
        + jnp.dot(mixed.T.astype(BF16), emit_ref[...], preferred_element_type=F32)
        + emit_bias_ref[...]
    )
    z = norm_rows(y, gain2_ref[...], bias2_ref[...])
    result = y + exit_bias_ref[...]
    chunk = x_ref.shape[1]
    for at in range(0, entry_ref.shape[1], chunk):
        h = jnp.dot(z, entry_ref[:, at : at + chunk], preferred_element_type=F32)
        g = exact_gelu(h + entry_bias_ref[:, at : at + chunk]).astype(BF16)
        result += jnp.dot(g, exit_ref[at : at + chunk], preferred_element_type=F32)
    out_ref[...] = result.astype(BF16)


def whole(array):
    return pl.BlockSpec(array.shape, lambda i: (0,) * array.ndim)


def body(
    layer_inputs_trainorder,
    inference_placement,
    initial_layernorm_gain,
    initial_layernorm_offset,
    attribute_projection,
    assignment_feeder_projection,
    partition_projection,
    partition_offset,
    softmax_sharpness,
    partition_question_map,
    partition_lookup_map,
    partition_content_map,
    emitted_projection,
    emitted_offset,
    latter_layernorm_gain,
    latter_layernorm_offset,
    perceptron_entry_map,
    perceptron_entry_offset,
    perceptron_exit_map,
    perceptron_exit_offset,
):
    groups = lax.axis_size("head")
    shards = lax.axis_size("pts")
    devices = groups * shards
    both = ("head", "pts")
    local_rows, width = layer_inputs_trainorder.shape
    per_pair = local_rows // devices
    own_heads = softmax_sharpness.shape[0]
    heads = own_heads * groups
    slices = partition_projection.shape[1]
    columns = heads * slices
    unit = per_pair // sum(SHARES)
    ends = [unit * sum(SHARES[: at + 1]) for at in range(len(SHARES))]
    spans = list(zip([0] + ends[:-1], ends))
    tile = math.gcd(TILE, *(high * devices for high in ends))

    dest_block = inference_placement // local_rows
    target = dest_block % groups * shards + dest_block // groups
    send_key = target * local_rows + inference_placement % local_rows
    counting = jnp.arange(local_rows, dtype=jnp.int32)
    send_key, ordering = lax.sort((send_key, counting), num_keys=1)
    ordering = ordering.reshape(devices, per_pair)
    spots = (send_key % local_rows).astype(F32).reshape(devices, per_pair)
    small = jnp.concatenate(
        [spots, jnp.broadcast_to(softmax_sharpness, (devices, own_heads))], axis=1
    )

    def gathered(order):
        return layer_inputs_trainorder[order.reshape(-1)]

    def exchange(rows):
        return lax.all_to_all(rows, both, split_axis=0, concat_axis=0, tiled=True)

    arrived = [exchange(gathered(ordering[:, : ends[0]]))]
    small = exchange(small)
    sharpness = small.reshape(groups, shards, -1)[:, 0, per_pair:].reshape(1, heads)
    arrived_spots = small[:, :per_pair].astype(jnp.int32)
    arrived_spots = jnp.concatenate(
        [arrived_spots[:, low:high].reshape(-1) for low, high in spans]
    )
    _, placed = lax.sort((arrived_spots, counting), num_keys=1)

    gain = initial_layernorm_gain[None]
    bias = initial_layernorm_offset[None]
    operands = (
        gain, bias, attribute_projection, assignment_feeder_projection, partition_projection,
        partition_offset[None], sharpness,
    )
    made = (
        jax.ShapeDtypeStruct((DH + 8, columns), F32),
        jax.ShapeDtypeStruct((2 * width, width), BF16),
        jax.ShapeDtypeStruct((columns, width), BF16),
        jax.ShapeDtypeStruct((columns, 1), F32),
        jax.ShapeDtypeStruct((columns, 1), F32),
    )
    sums, *constants = pl.pallas_call(
        functools.partial(sums_kernel, slices),
        grid=(local_rows // tile,),
        in_specs=[pl.BlockSpec((tile, width), lambda i: (i, 0))] + [whole(a) for a in operands],
        out_specs=[whole(a) for a in made],
        out_shape=made,
        scratch_shapes=[pltpu.VMEM((width, columns), F32), pltpu.VMEM((columns, 128), F32)],
        compiler_params=pltpu.CompilerParams(dimension_semantics=("arbitrary",)),
        cost_estimate=pl.CostEstimate(
            flops=local_rows * width * columns * 8, bytes_accessed=local_rows * width * 16,
            transcendentals=local_rows * columns,
        ),
    )(layer_inputs_trainorder, *operands)

    waiting, sums, arrived[0] = lax.optimization_barrier(
        (gathered(ordering[:, ends[0] : ends[1]]), sums, arrived[0])
    )
    part = jnp.sum(exchange(sums.reshape(devices, -1)), axis=0)
    sums = exchange(jnp.broadcast_to(part, (devices,) + part.shape)).reshape(sums.shape)
    waiting, later, sums = lax.optimization_barrier((waiting, ordering, sums))
    arrived.append(exchange(waiting))
    later = [gathered(later[:, low:high]) for low, high in spans[2:]]

    maps = (sums, partition_question_map, partition_lookup_map, partition_content_map)
    blend = pl.pallas_call(
        functools.partial(blend_kernel, slices),
        out_shape=jax.ShapeDtypeStruct((width, columns), BF16),
        cost_estimate=pl.CostEstimate(
            flops=columns * columns * 1000, bytes_accessed=columns * width * 8,
            transcendentals=columns * columns,
        ),
    )(*maps)

    operands = (
        blend, gain, bias, *constants, emitted_projection,
        emitted_offset[None], latter_layernorm_gain[None], latter_layernorm_offset[None],
        perceptron_entry_map, perceptron_entry_offset[None], perceptron_exit_map,
        perceptron_exit_offset[None],
    )
    result = ()
    for at, (low, high) in enumerate(spans):
        chunk_rows = (high - low) * devices
        first = low * devices // tile
        result = pl.pallas_call(
            functools.partial(rows_kernel, slices),
            grid=(chunk_rows // tile,),
            in_specs=[pl.BlockSpec((tile, width), lambda i: (i, 0))]
            + [whole(a) for a in operands]
            + [pl.BlockSpec(memory_space=pl.ANY) for _ in result],
            out_specs=(pl.BlockSpec((tile, width), lambda i, first=first: (i + first, 0)),),
            out_shape=(jax.ShapeDtypeStruct((local_rows, width), BF16),),
            input_output_aliases={1 + len(operands): 0} if result else {},
            compiler_params=pltpu.CompilerParams(dimension_semantics=("arbitrary",)),
            cost_estimate=pl.CostEstimate(
                flops=chunk_rows * width * columns * 16, bytes_accessed=chunk_rows * width * 16,
                transcendentals=chunk_rows * columns * 4,
            ),
        )(arrived[at], *operands, *result)
        if at + 2 < len(SHARES):
            leaving, result = lax.optimization_barrier((later[at], result))
            arrived.append(exchange(leaving))
    return result[0][placed][None]


def solution(mesh):
    placed = (
        P(("head", "pts"), None),
        P(("head", "pts")),
        P(),
        P(),
        P(),
        P(),
        P(),
        P(),
        P("head"),
        P(),
        P(),
        P(),
        P(),
        P(),
        P(),
        P(),
        P(),
        P(),
        P(),
        P(),
    )
    return jax.shard_map(
        body, mesh=mesh, in_specs=placed, out_specs=P("pts", "head", None), check_vma=False
    )
```

profile of v0, /device:TPU:0, one launch (start us, length us, event | category | flops | bytes accessed | tf_op | source)
XLA Modules:
  0.0 174.6 jit_solution(1362965709390596040)
XLA Ops:
  0.0 0.8 fusion.3
  0.8 6.2 %sort.30 = (s32[6144]{0:T(1024)S(1)}, s32[6144]{0:T(1024)S(1)}) sort(s32[6144]{0:T(1024)S(1)} %fusion.3, s32[6144]{0:T(1024)S(1)} %iota.5), dimensions={0}, to_apply=%region_0.1 | sort | flops 79872 | bytes 98304 | tf_op jit(solution)/shard_map/sort | solution.py:192
  7.1 0.7 pad.4.clone
  7.9 0.6 all_to_all.40
  8.5 7.3 %all-to-all-start = ((f32[32,1,196]{2,1,0:T(1,128)}), f32[32,1,196]{2,1,0:T(1,128)S(1)}, u32[]{:S(2)}, u32[]{:S(2)}) async-start(f32[32,1,196]{2,1,0:T(1,128)} %all_to_all.40), calls=%async_computation | async-start | bytes 65536 | tf_op jit(solution)/shard_map/all_to_all | solution.py:203
  15.9 0.1 reshape.136
  16.1 9.3 %gather_fusion.1 = bf16[2560,256]{1,0:T(8,128)(2,1)} fusion(bf16[6144,256]{1,0:T(8,128)(2,1)} %x_ref.1, s32[3072]{0:T(1024)S(1)} %pad_clamp_fusion), kind=kCustom, calls=%fused_computation.1 | custom fusion | bytes 2631680 | tf_op jit(solution)/shard_map/gather | solution.py:200
  25.3 5.9 %all-to-all-start.1 = ((bf16[32,80,256]{2,1,0:T(8,128)(2,1)}), bf16[32,80,256]{2,1,0:T(8,128)(2,1)}, u32[]{:S(2)}, u32[]{:S(2)}) async-start(bf16[32,80,256]{2,1,0:T(8,128)(2,1)} %bitcast.21), calls=%async_computation.1 | async-start | bytes 2621440 | tf_op jit(solution)/shard_map/all_to_all | solution.py:203
  31.3 0.1 reshape.133
  31.5 9.0 %gather_fusion = bf16[2048,256]{1,0:T(8,128)(2,1)} fusion(bf16[6144,256]{1,0:T(8,128)(2,1)S(1)} %copy-done, s32[2048]{0:T(1024)S(1)} %broadcast_clamp_fusion), kind=kCustom, calls=%fused_computation | custom fusion | bytes 2105344 | tf_op jit(solution)/shard_map/gather | solution.py:200
  40.4 0.1 slice_reduce_fusion
  40.5 0.6 reshape_squeeze.3.sharp_row_ref
  41.2 18.6 %shard_map.190 = (f32[24,512]{1,0:T(8,128)}, bf16[512,256]{1,0:T(8,128)(2,1)}, bf16[512,256]{1,0:T(8,128)(2,1)}, f32[512,1]{1,0:T(8,128)}, f32[512,1]{1,0:T(8,128)}) custom-call(bf16[6144,256]{1,0:T(8,128)(2,1)} %x_ref.1, f32[1,256]{1,0:T(1,128)} %bitcast.30, f32[1,256]{1,0:T(1,128)} %bitcast.34, bf16[256,256]{1,0:T(8,128)(2,1)} %attribute_ref.1, ...), custom_call_target="tpu_custom_call" | custom-call | flops 6442450944 | bytes 25165824 | tf_op jit(solution)/shard_map/pallas_call | solution.py:227
  59.8 3.4 %all-to-all-done.1 = bf16[32,80,256]{2,1,0:T(8,128)(2,1)} async-done(((bf16[32,80,256]{2,1,0:T(8,128)(2,1)}), bf16[32,80,256]{2,1,0:T(8,128)(2,1)}, u32[]{:S(2)}, u32[]{:S(2)}) %all-to-all-start.1) | async-done | bytes 1310752 | tf_op jit(solution)/shard_map/all_to_all | solution.py:203
  63.2 0.9 all_to_all.55
  64.1 10.7 %all_to_all.62 = f32[32,1,384]{2,1,0:T(1,128)S(1)} all-to-all(f32[32,1,384]{2,1,0:T(1,128)S(1)} %all_to_all.55), channel_id=1, replica_groups=mesh['head'=4,'pts'=8] {'head','pts'}, dimensions={0} | all-to-all | bytes 98304 | tf_op jit(solution)/shard_map/all_to_all | solution.py:203
  74.9 9.0 %all_to_all.63 = f32[32,1,384]{2,1,0:T(1,128)S(1)} all-to-all(f32[32,1,384]{2,1,0:T(1,128)S(1)} %broadcast_in_dim.43), channel_id=1, replica_groups=mesh['head'=4,'pts'=8] {'head','pts'}, dimensions={0} | all-to-all | bytes 98304 | tf_op jit(solution)/shard_map/all_to_all | solution.py:203
  83.9 0.1 reduce.3
  84.0 0.6 reshape.137.sums_ref
  84.7 3.4 %all-to-all-start.5 = ((bf16[32,64,256]{2,1,0:T(8,128)(2,1)}), bf16[32,64,256]{2,1,0:T(8,128)(2,1)}, u32[]{:S(2)}, u32[]{:S(2)}) async-start(bf16[32,64,256]{2,1,0:T(8,128)(2,1)} %bitcast.22), calls=%async_computation.5 | async-start | bytes 2097152 | tf_op jit(solution)/shard_map/all_to_all | solution.py:203
  88.1 0.1 reshape.138
  88.3 5.4 %gather_fusion.2 = bf16[1536,256]{1,0:T(8,128)(2,1)} fusion(bf16[6144,256]{1,0:T(8,128)(2,1)S(1)} %copy-done.1, s32[2048]{0:T(1024)S(1)} %pad_clamp_fusion.1), kind=kCustom, calls=%fused_computation.2 | custom fusion | bytes 1579008 | tf_op jit(solution)/shard_map/gather | solution.py:200
  93.6 3.5 %shard_map.191.blend = bf16[256,512]{1,0:T(8,128)(2,1)} custom-call(f32[24,512]{1,0:T(8,128)} %reshape.137.sums_ref, f32[16,16]{1,0:T(8,128)} %question_ref.1, f32[16,16]{1,0:T(8,128)} %lookup_ref.1, f32[16,16]{1,0:T(8,128)} %content_ref.1), custom_call_target="tpu_custom_call" | custom-call | flops 262144000 | bytes 1048576 | tf_op jit(solution)/shard_map/pallas_call | solution.py:251
  97.1 14.2 %shard_map.192.earlier_and_out_0_ = bf16[6144,256]{1,0:T(8,128)(2,1)} custom-call(bf16[2560,256]{1,0:T(8,128)(2,1)} %bitcast.5.x_ref, bf16[256,512]{1,0:T(8,128)(2,1)} %shard_map.191.blend, f32[1,256]{1,0:T(1,128)} %bitcast.31, f32[1,256]{1,0:T(1,128)} %bitcast.35, bf16[512,256]{1,0:T(8,128)(2,1)} %get-tuple-element.29.w_ref, ...), custom_call_target="tpu_custom_call" | custom-call | flops 5368709120 | bytes 10485760 | tf_op jit(solution)/shard_map/pallas_call | solution.py:270
  111.4 2.8 %all-to-all-done.5 = bf16[32,64,256]{2,1,0:T(8,128)(2,1)} async-done(((bf16[32,64,256]{2,1,0:T(8,128)(2,1)}), bf16[32,64,256]{2,1,0:T(8,128)(2,1)}, u32[]{:S(2)}, u32[]{:S(2)}) %all-to-all-start.5) | async-done | bytes 1048608 | tf_op jit(solution)/shard_map/all_to_all | solution.py:203
  114.2 3.5 %all-to-all-start.4 = ((bf16[32,48,256]{2,1,0:T(8,128)(2,1)}), bf16[32,48,256]{2,1,0:T(8,128)(2,1)S(1)}, u32[]{:S(2)}, u32[]{:S(2)}) async-start(bf16[32,48,256]{2,1,0:T(8,128)(2,1)} %bitcast.11), calls=%async_computation.4 | async-start | bytes 1572864 | tf_op jit(solution)/shard_map/all_to_all | solution.py:203
  118.2 6.7 %sort.31 = (s32[6144]{0:T(1024)}, s32[6144]{0:T(1024)S(1)}) sort(s32[6144]{0:T(1024)S(1)} %pad_add_fusion, s32[6144]{0:T(1024)S(1)} %iota.6), dimensions={0}, to_apply=%region_2.3 | sort | flops 79872 | bytes 98304 | tf_op jit(solution)/shard_map/sort | solution.py:212
  124.9 11.9 %shard_map.193.earlier_and_out_0_ = bf16[6144,256]{1,0:T(8,128)(2,1)} custom-call(bf16[2048,256]{1,0:T(8,128)(2,1)} %bitcast.14.x_ref, bf16[256,512]{1,0:T(8,128)(2,1)} %shard_map.191.blend, f32[1,256]{1,0:T(1,128)} %bitcast.32, f32[1,256]{1,0:T(1,128)} %bitcast.36, bf16[512,256]{1,0:T(8,128)(2,1)} %get-tuple-element.29.w_ref, ...), custom_call_target="tpu_custom_call", output_to_operand_aliasing={{}: (16, {})} | custom-call | flops 4294967296 | bytes 8388608 | tf_op jit(solution)/shard_map/pallas_call | solution.py:270
  136.9 1.5 all-to-all-done.4
  138.4 0.9 copy-done.2
  139.2 9.5 %shard_map.194 = bf16[6144,256]{1,0:T(8,128)(2,1)} custom-call(bf16[1536,256]{1,0:T(8,128)(2,1)} %bitcast.23, bf16[256,512]{1,0:T(8,128)(2,1)} %shard_map.191.blend, f32[1,256]{1,0:T(1,128)} %bitcast.33, f32[1,256]{1,0:T(1,128)} %bitcast.37, bf16[512,256]{1,0:T(8,128)(2,1)} %get-tuple-element.29.w_ref, ...), custom_call_target="tpu_custom_call", output_to_operand_aliasing={{}: (16, {})} | custom-call | flops 3221225472 | bytes 6291456 | tf_op jit(solution)/shard_map/pallas_call | solution.py:270
  148.8 25.8 %gather_fusion.3 = bf16[6144,256]{1,0:T(8,128)(2,1)} fusion(bf16[6144,256]{1,0:T(8,128)(2,1)} %shard_map.194, s32[6144]{0:T(1024)S(1)} %fusion.5), kind=kCustom, calls=%fused_computation.3 | custom fusion | bytes 6316032 | tf_op jit(solution)/shard_map/gather | solution.py:288
  (33 shorter events, 0.9 us)
Async XLA Ops:
  8.5 16.8 %all-to-all-start = ((f32[32,1,196]{2,1,0:T(1,128)}), f32[32,1,196]{2,1,0:T(1,128)S(1)}, u32[]{:S(2)}, u32[]{:S(2)}) async-start(f32[32,1,196]{2,1,0:T(1,128)} %all_to_all.40), calls=%async_computation | async-start | bytes 65536 | tf_op jit(solution)/shard_map/all_to_all | solution.py:203
  16.0 15.4 %copy-start = (bf16[6144,256]{1,0:T(8,128)(2,1)S(1)}, bf16[6144,256]{1,0:T(8,128)(2,1)}, u32[]{:S(2)}) copy-start(bf16[6144,256]{1,0:T(8,128)(2,1)} %x_ref.1) | copy-start | bytes 9437188
  25.3 37.9 %all-to-all-start.1 = ((bf16[32,80,256]{2,1,0:T(8,128)(2,1)}), bf16[32,80,256]{2,1,0:T(8,128)(2,1)}, u32[]{:S(2)}, u32[]{:S(2)}) async-start(bf16[32,80,256]{2,1,0:T(8,128)(2,1)} %bitcast.21), calls=%async_computation.1 | async-start | bytes 2621440 | tf_op jit(solution)/shard_map/all_to_all | solution.py:203
  41.2 47.1 %copy-start.1 = (bf16[6144,256]{1,0:T(8,128)(2,1)S(1)}, bf16[6144,256]{1,0:T(8,128)(2,1)}, u32[]{:S(2)}) copy-start(bf16[6144,256]{1,0:T(8,128)(2,1)} %x_ref.1) | copy-start | bytes 9437188
  84.7 29.6 %all-to-all-start.5 = ((bf16[32,64,256]{2,1,0:T(8,128)(2,1)}), bf16[32,64,256]{2,1,0:T(8,128)(2,1)}, u32[]{:S(2)}, u32[]{:S(2)}) async-start(bf16[32,64,256]{2,1,0:T(8,128)(2,1)} %bitcast.22), calls=%async_computation.5 | async-start | bytes 2097152 | tf_op jit(solution)/shard_map/all_to_all | solution.py:203
  114.2 24.1 %all-to-all-start.4 = ((bf16[32,48,256]{2,1,0:T(8,128)(2,1)}), bf16[32,48,256]{2,1,0:T(8,128)(2,1)S(1)}, u32[]{:S(2)}, u32[]{:S(2)}) async-start(bf16[32,48,256]{2,1,0:T(8,128)(2,1)} %bitcast.11), calls=%async_computation.4 | async-start | bytes 1572864 | tf_op jit(solution)/shard_map/all_to_all | solution.py:203
  138.4 0.9 copy-start.2
where the time goes:
time: 175 us
  Pallas kernels  57.8 us (33%)
  local copies, waits for them, and re-layouts  54.9 us (31%)
  starting transfers between devices  20.2 us (12%)
  blocking collectives  19.8 us (11%)
  other arithmetic  14 us (8%)
  waiting for transfers between devices  7.71 us (4%)
    pallas_call x3, Pallas kernels, body(): pl.pallas_call(functools.partial(rows_kernel, slices), grid=(chunk_rows /...  35.7 us
    gather x1, local copies, waits for them, and re-layouts, body(): return result[0][placed][None]  25.8 us
    gather x3, local copies, waits for them, and re-layouts, gathered(): return layer_inputs_trainorder[order.reshape(-1)]  23.6 us
    all_to_all x4, starting transfers between devices, exchange(): return lax.all_to_all(rows, both, split_axis=0, concat_axis=0, tiled=True)  20.2 us
    all_to_all x2, blocking collectives, exchange(): return lax.all_to_all(rows, both, split_axis=0, concat_axis=0, tiled=True)  19.8 us
    pallas_call x1, Pallas kernels, body(): pl.pallas_call(functools.partial(sums_kernel, slices), grid=(local_rows /...  18.6 us
    all_to_all x4, waiting for transfers between devices, exchange(): return lax.all_to_all(rows, both, split_axis=0, concat_axis=0, tiled=True)  7.71 us
    sort x1, other arithmetic, body(): _, placed = lax.sort((arrived_spots, counting), num_keys=1)  6.72 us
  transfers between devices with their start and end apart: 4, of which 3 were waited for; matrix products, arithmetic and copies ran while one was open for 18% of the time, Pallas kernels for 28%

commit v1 on v0

v1 whole, which is shorter than its diff:
```python
import functools
import math

import jax
import jax.numpy as jnp
from jax import lax
from jax.experimental import pallas as pl
from jax.experimental.pallas import tpu as pltpu
from jax.sharding import PartitionSpec as P

DH = 16
LANES = 128
STEPS = 16
EARLY = 12
F32 = jnp.float32
BF16 = jnp.bfloat16
I32 = jnp.int32
HIGHEST = lax.Precision.HIGHEST
LOG2E = math.log2(math.e)
NT = (((1,), (1,)), ((), ()))
MESH = pl.DeviceIdType.MESH


def norm_rows(rows, gain, bias):
    mean = jnp.mean(rows, axis=-1, keepdims=True)
    centred = rows - mean
    spread = jnp.mean(centred * centred, axis=-1, keepdims=True)
    return (centred * lax.rsqrt(spread + 1e-05) * gain + bias).astype(BF16)


def slice_weights(feeder_t, expand, offset, scale, slices):
    raw = jnp.dot(expand, feeder_t, preferred_element_type=F32)
    logit = (raw + offset) * scale
    lanes = logit.shape[1]
    logit = logit.reshape(-1, slices, lanes)
    powers = jnp.exp2(logit - jnp.max(logit, axis=1, keepdims=True))
    share = powers * (1.0 / jnp.sum(powers, axis=1, keepdims=True))
    return share.reshape(-1, lanes)


def same_head(shape, row_size, column_size):
    row_head = lax.broadcasted_iota(I32, shape, 0) // row_size
    column_head = lax.broadcasted_iota(I32, shape, 1) // column_size
    return row_head == column_head


def exact_gelu(h):
    half = 0.5 * h
    return half + half * lax.erf(h * (1.0 / math.sqrt(2.0)))


def floor_div(value, divisor):
    return ((value.astype(F32) + 0.5) * (1.0 / divisor)).astype(I32)


def flip(a, b, size):
    result, bit = 0, 1
    while bit < size:
        result = result + (a // bit + b // bit) % 2 * bit
        bit *= 2
    return result


def index_kernel(groups, shards, rows, place_ref, order_ref, spots_ref, rank_v, target_v, spot_v):
    devices = groups * shards
    chunks = rows // LANES

    place = place_ref[...]
    block = floor_div(place, rows)
    shard = floor_div(block, groups)
    target = (block - shard * groups) * shards + shard
    target_v[...] = target
    spot_v[...] = place - block * rows
    upper = (
        lax.broadcasted_iota(I32, (LANES, LANES), 0) <= lax.broadcasted_iota(I32, (LANES, LANES), 1)
    ).astype(F32).astype(BF16)
    stacked = jnp.concatenate(
        [
            (lax.broadcasted_iota(I32, (devices, LANES), 0)
             == target[:, at * LANES : (at + 1) * LANES]).astype(F32)
            for at in range(chunks)
        ],
        axis=0,
    )
    prefix = jnp.dot(stacked.astype(BF16), upper, preferred_element_type=F32)
    run = jnp.zeros((devices, 1), F32)
    for at in range(chunks):
        span = slice(at * devices, (at + 1) * devices)
        ahead = jnp.sum(stacked[span] * (prefix[span] + (run - 1.0)), axis=0, keepdims=True)
        rank_v[:, at * LANES : (at + 1) * LANES] = ahead.astype(I32)
        run = run + prefix[span][:, LANES - 1 :]

    wide = order_ref.shape[1]
    part_lanes = 4 * LANES

    def invert(at, total_so_far):
        lanes = pl.ds(pl.multiple_of(at * part_lanes, part_lanes), part_lanes)
        hot = (
            lax.broadcasted_iota(I32, (devices, part_lanes), 0) == target_v[:, lanes]
        ).astype(F32)
        slot_hot = (
            lax.broadcasted_iota(I32, (wide, part_lanes), 0) == rank_v[:, lanes]
        ).astype(F32).astype(BF16)
        index = lax.broadcasted_iota(I32, (1, part_lanes), 1) + at * part_lanes
        values = []
        for value in (index, spot_v[:, lanes]):
            high = value // 64
            values += [hot * high.astype(F32), hot * (value - high * 64).astype(F32)]
        values = jnp.concatenate(values, axis=0).astype(BF16)
        return total_so_far + lax.dot_general(values, slot_hot, NT, preferred_element_type=F32)

    table = lax.fori_loop(
        0, rows // part_lanes, invert, jnp.zeros((4 * devices, wide), F32)
    )
    order_ref[...] = (table[:devices] * 64.0 + table[devices : 2 * devices]).astype(I32)
    spots = table[2 * devices : 3 * devices] * 64.0 + table[3 * devices :]
    for at in range(devices):
        spots_ref[at] = spots[at : at + 1].astype(I32)


def fused_kernel(
    slices, groups, shards,
    x_hbm, order_s, meta_v, sharp_ref, gain_ref, bias_ref, attribute_ref, feeder_ref, project_ref,
    offset_row_ref, question_ref, lookup_ref, content_ref, emit_ref, emit_bias_ref,
    gain2_ref, bias2_ref, entry_ref, entry_bias_ref, exit_ref, exit_bias_ref,
    res_hbm, meta_in,
    x_v, xf, stage, send_v, recv_v, res,
    sharp_v, sharp_in, w_ref, expand_ref, offset_ref, scale_ref, numer, total,
    part_out, part_in, mine, all_in, sums_v, blend,
    local_sem, out_sem, row_send, row_recv, meta_send, meta_recv, sharp_send, sharp_recv,
    part_send, part_recv, all_send, all_recv,
):
    devices = groups * shards
    rows, width = x_v.shape
    per_pair = rows // devices
    tile = rows // STEPS
    blocks = devices // STEPS
    columns = expand_ref.shape[0]
    own = sharp_ref.shape[1]
    my_head, my_pts = lax.axis_index("head"), lax.axis_index("pts")
    me = my_head * shards + my_pts

    def peer(slot):
        return flip(my_head, slot % groups, groups), flip(my_pts, slot // groups, shards)

    def flat(slot):
        head, pts = peer(slot)
        return head * shards + pts

    def loop(low, high, step):
        def run(at, carry):
            step(at)
            return carry
        lax.fori_loop(low, high, run, 0)

    barrier = pltpu.get_barrier_semaphore()
    loop(1, devices, lambda slot: pl.semaphore_signal(
        barrier, 1, device_id=peer(slot), device_id_type=MESH
    ))
    load = pltpu.make_async_copy(x_hbm, x_v, local_sem.at[0])
    load.start()

    sharp_v[...] = jnp.zeros_like(sharp_v)
    sharp_v[:, :own] = sharp_ref[...]
    sharp_in[my_head] = sharp_v[...]

    w_ref[:width] = attribute_ref[...].astype(F32).T.astype(BF16)
    w_ref[width:] = feeder_ref[...].astype(F32).T.astype(BF16)
    repeated = jnp.concatenate([project_ref[...].astype(F32).T] * (columns // slices), axis=0)
    lane = lax.broadcasted_iota(I32, (DH, width), 1) % DH
    pick = (lane == lax.broadcasted_iota(I32, (DH, width), 0)).astype(F32).astype(BF16)
    filled = jnp.dot(repeated.astype(BF16), pick, preferred_element_type=F32)
    expand_ref[...] = jnp.where(same_head(filled.shape, slices, DH), filled, 0.0).astype(BF16)
    row = lax.broadcasted_iota(I32, (columns, slices), 0) % slices
    match = row == lax.broadcasted_iota(I32, (columns, slices), 1)
    offset_ref[...] = jnp.sum(jnp.where(match, offset_row_ref[...], 0.0), axis=1, keepdims=True)
    numer[...] = jnp.zeros_like(numer)
    total[...] = jnp.zeros_like(total)

    pl.semaphore_wait(barrier, devices - 1)

    def sharp_copy(step):
        return pltpu.make_async_remote_copy(
            sharp_v, sharp_in.at[my_head], sharp_send.at[step], sharp_recv.at[step],
            device_id=(flip(my_head, step, groups), my_pts), device_id_type=MESH,
        )

    def meta_copy(slot):
        return pltpu.make_async_remote_copy(
            meta_v.at[flat(slot)], meta_in.at[slot], meta_send.at[slot], meta_recv.at[slot],
            device_id=peer(slot), device_id_type=MESH,
        )

    def row_copy(slot):
        span = pl.ds(pl.multiple_of(slot * per_pair, per_pair), per_pair)
        return pltpu.make_async_remote_copy(
            send_v.at[span], recv_v.at[span], row_send.at[slot], row_recv.at[slot],
            device_id=peer(slot), device_id_type=MESH,
        )

    def part_copy(slot):
        return pltpu.make_async_remote_copy(
            part_out.at[flat(slot)], part_in.at[slot], part_send.at[slot], part_recv.at[slot],
            device_id=peer(slot), device_id_type=MESH,
        )

    def all_copy(slot):
        return pltpu.make_async_remote_copy(
            mine, all_in.at[me], all_send.at[slot], all_recv.at[slot],
            device_id=peer(slot), device_id_type=MESH,
        )

    loop(1, groups, lambda step: sharp_copy(step).start())
    loop(1, devices, lambda slot: meta_copy(slot).start())
    meta_in[0] = meta_v[me]

    load.wait()

    def widen(at):
        part = x_v[pl.ds(pl.multiple_of(at * tile, tile), tile), :].astype(F32)
        xf[pl.ds(at * 2 * tile, tile, stride=2), :] = part[:, :LANES]
        xf[pl.ds(at * 2 * tile + 1, tile, stride=2), :] = part[:, LANES:]

    loop(0, STEPS, widen)
    loop(1, groups, lambda step: sharp_copy(step).wait())
    per_group = own * slices
    for group in range(groups):
        lane = lax.broadcasted_iota(I32, (per_group, LANES), 1)
        member = lax.broadcasted_iota(I32, (per_group, LANES), 0) // slices
        sharp = jnp.sum(jnp.where(lane == member, sharp_in[group], 0.0), axis=1, keepdims=True)
        scale_ref[group * per_group : (group + 1) * per_group] = LOG2E / sharp

    def sums_step(at):
        @pl.when(jnp.logical_and(at > 0, at <= EARLY // blocks))
        def _():
            for way in range(blocks):
                slot = (at - 1) * blocks + way

                @pl.when(slot > 0)
                def _():
                    row_copy(slot).start()

        for way in range(blocks):
            goal = flat(at * blocks + way)
            for k in range(per_pair):
                put = 2 * (way * per_pair + k)
                stage[put : put + 2, :] = xf[pl.ds(order_s[goal, k] * 2, 2), :]
        span = pl.ds(pl.multiple_of(at * tile, tile), tile)
        send_v[span, :LANES] = stage[pl.ds(0, tile, stride=2), :].astype(BF16)
        send_v[span, LANES:] = stage[pl.ds(1, tile, stride=2), :].astype(BF16)

        normed = norm_rows(x_v[span, :].astype(F32), gain_ref[...], bias_ref[...])
        both = lax.dot_general(w_ref[...], normed, NT, preferred_element_type=F32).astype(BF16)
        share = slice_weights(
            both[width:], expand_ref[...], offset_ref[...], scale_ref[...], slices
        )
        numer[...] += lax.dot_general(
            both[:width], share.astype(BF16), NT, preferred_element_type=F32
        )
        part = share[:, :LANES]
        for low in range(LANES, tile, LANES):
            part += share[:, low : low + LANES]
        total[...] += part

    loop(0, STEPS, sums_step)

    kept = jnp.where(same_head(numer.shape, DH, slices), numer[...], 0.0)
    sums_v[:DH] = jnp.sum(kept.reshape(-1, DH, columns), axis=0)
    sums_v[DH:] = lax.dot_general(
        jnp.ones((8, LANES), F32), total[...], NT, precision=HIGHEST, preferred_element_type=F32
    )
    per_row = columns // LANES
    depth = part_out.shape[1]
    places = [
        (at // per_row, at % per_row * LANES, at // depth, at % depth)
        for at in range((DH + 1) * per_row)
    ]
    part_out[...] = jnp.zeros_like(part_out)
    for line, low, piece, inner in places:
        part_out[piece, inner : inner + 1, :] = sums_v[line : line + 1, low : low + LANES]
    loop(1, devices, lambda slot: part_copy(slot).start())
    part_in[0] = part_out[me]
    loop(max(EARLY, 1), devices, lambda slot: row_copy(slot).start())

    loop(1, devices, lambda slot: part_copy(slot).wait())
    mine[...] = jnp.sum(part_in[...], axis=0)
    loop(1, devices, lambda slot: all_copy(slot).start())
    all_in[me] = mine[...]
    loop(1, devices, lambda slot: all_copy(slot).wait())
    for line, low, piece, inner in places:
        sums_v[line : line + 1, low : low + LANES] = all_in[piece, inner : inner + 1, :]

    stok = sums_v[:DH] / (sums_v[DH : DH + 1] + 1e-05)
    query, key, value = (
        jnp.dot(m[...].T, stok, precision=HIGHEST, preferred_element_type=F32)
        for m in (question_ref, lookup_ref, content_ref)
    )
    scores = jnp.dot(key.T, query, precision=HIGHEST, preferred_element_type=F32)
    scores = scores * (1.0 / math.sqrt(DH))
    mask = same_head(scores.shape, slices, slices)
    scores = jnp.where(mask, scores, -jnp.inf)
    powers = jnp.exp(scores - jnp.max(scores, axis=0, keepdims=True))
    attention = powers / jnp.sum(powers, axis=0, keepdims=True)
    sout = jnp.dot(value, attention, precision=HIGHEST, preferred_element_type=F32)
    spread = jnp.concatenate([sout] * (width // DH), axis=0)
    blend[...] = jnp.where(same_head(blend.shape, DH, slices), spread, 0.0).astype(BF16)
    recv_v[:per_pair] = send_v[:per_pair]

    def rows_step(at):
        def arrived(way):
            slot = at * blocks + way

            @pl.when(slot > 0)
            def _():
                row_copy(slot).wait_recv()

        loop(0, blocks, arrived)
        x = recv_v[pl.ds(pl.multiple_of(at * tile, tile), tile), :].astype(F32)
        normed = norm_rows(x, gain_ref[...], bias_ref[...])
        feeder = lax.dot_general(
            w_ref[width:], normed, NT, preferred_element_type=F32
        ).astype(BF16)
        share = slice_weights(feeder, expand_ref[...], offset_ref[...], scale_ref[...], slices)
        mixed = jnp.dot(blend[...], share.astype(BF16), preferred_element_type=F32)
        y = (
            x
            + jnp.dot(mixed.T.astype(BF16), emit_ref[...], preferred_element_type=F32)
            + emit_bias_ref[...]
        )
        z = norm_rows(y, gain2_ref[...], bias2_ref[...])
        result = y + exit_bias_ref[...]
        for low in range(0, entry_ref.shape[1], width):
            h = jnp.dot(z, entry_ref[:, low : low + width], preferred_element_type=F32)
            g = exact_gelu(h + entry_bias_ref[:, low : low + width]).astype(BF16)
            result += jnp.dot(g, exit_ref[low : low + width], preferred_element_type=F32)
        res[pl.ds(at * 2 * tile, tile, stride=2), :] = result[:, :LANES]
        res[pl.ds(at * 2 * tile + 1, tile, stride=2), :] = result[:, LANES:]
        out_copy(at).start()

    def out_copy(at):
        span = pl.ds(pl.multiple_of(at * 2 * tile, 2 * tile), 2 * tile)
        return pltpu.make_async_copy(res.at[span], res_hbm.at[span], out_sem.at[at])

    loop(0, STEPS, rows_step)
    loop(1, devices, lambda slot: meta_copy(slot).wait())
    loop(1, devices, lambda slot: row_copy(slot).wait_send())
    loop(0, STEPS, lambda at: out_copy(at).wait())


def serve_kernel(spot_s, res_ref, out_ref, placed):
    step = pl.program_id(0)
    tile = res_ref.shape[0] // 2
    blocks = spot_s.shape[0] // pl.num_programs(0)
    per_pair = tile // blocks
    for way in range(blocks):
        for k in range(per_pair):
            spot = spot_s[step * blocks + way, 0, k]
            at = 2 * (way * per_pair + k)
            placed[pl.ds(pl.multiple_of(spot * 2, 2), 2), :] = res_ref[at : at + 2, :]

    @pl.when(step == pl.num_programs(0) - 1)
    def _():
        def narrow(at, carry):
            span = pl.ds(pl.multiple_of(at * tile, tile), tile)
            out_ref[span, :LANES] = placed[pl.ds(at * 2 * tile, tile, stride=2), :].astype(BF16)
            out_ref[span, LANES:] = placed[pl.ds(at * 2 * tile + 1, tile, stride=2), :].astype(
                BF16
            )
            return carry
        lax.fori_loop(0, out_ref.shape[0] // tile, narrow, 0)


def body(
    layer_inputs_trainorder,
    inference_placement,
    initial_layernorm_gain,
    initial_layernorm_offset,
    attribute_projection,
    assignment_feeder_projection,
    partition_projection,
    partition_offset,
    softmax_sharpness,
    partition_question_map,
    partition_lookup_map,
    partition_content_map,
    emitted_projection,
    emitted_offset,
    latter_layernorm_gain,
    latter_layernorm_offset,
    perceptron_entry_map,
    perceptron_entry_offset,
    perceptron_exit_map,
    perceptron_exit_offset,
):
    groups = lax.axis_size("head")
    shards = lax.axis_size("pts")
    devices = groups * shards
    rows, width = layer_inputs_trainorder.shape
    per_pair = rows // devices
    slices = partition_projection.shape[1]
    columns = softmax_sharpness.shape[0] * groups * slices
    wide = -(-per_pair // LANES) * LANES
    tile = rows // STEPS
    depth = -(-(DH + 1) * (columns // LANES) // devices)
    order, spots = pl.pallas_call(
        functools.partial(index_kernel, groups, shards, rows),
        out_shape=(
            jax.ShapeDtypeStruct((devices, wide), I32),
            jax.ShapeDtypeStruct((devices, 1, wide), I32),
        ),
        scratch_shapes=[pltpu.VMEM((1, rows), I32)] * 3,
    )(inference_placement[None])
    operands = (
        order, spots, softmax_sharpness[None], initial_layernorm_gain[None],
        initial_layernorm_offset[None], attribute_projection, assignment_feeder_projection,
        partition_projection, partition_offset[None], partition_question_map,
        partition_lookup_map, partition_content_map, emitted_projection, emitted_offset[None],
        latter_layernorm_gain[None], latter_layernorm_offset[None], perceptron_entry_map,
        perceptron_entry_offset[None], perceptron_exit_map, perceptron_exit_offset[None],
    )
    dma = pltpu.SemaphoreType.DMA
    scratch = [
        pltpu.VMEM((rows, width), BF16),
        pltpu.VMEM((2 * rows, LANES), F32),
        pltpu.VMEM((2 * tile, LANES), F32),
        pltpu.VMEM((rows, width), BF16),
        pltpu.VMEM((rows, width), BF16),
        pltpu.VMEM((2 * rows, LANES), F32),
        pltpu.VMEM((1, LANES), F32),
        pltpu.VMEM((groups, 1, LANES), F32),
        pltpu.VMEM((2 * width, width), BF16),
        pltpu.VMEM((columns, width), BF16),
        pltpu.VMEM((columns, 1), F32),
        pltpu.VMEM((columns, 1), F32),
        pltpu.VMEM((width, columns), F32),
        pltpu.VMEM((columns, LANES), F32),
        pltpu.VMEM((devices, depth, LANES), F32),
        pltpu.VMEM((devices, depth, LANES), F32),
        pltpu.VMEM((depth, LANES), F32),
        pltpu.VMEM((devices, depth, LANES), F32),
        pltpu.VMEM((DH + 8, columns), F32),
        pltpu.VMEM((width, columns), BF16),
        dma((2,)),
        dma((STEPS,)),
        dma((devices,)),
        dma((devices,)),
        dma((devices,)),
        dma((devices,)),
        dma((groups,)),
        dma((groups,)),
        dma((devices,)),
        dma((devices,)),
        dma((devices,)),
        dma((devices,)),
    ]
    in_vmem = pl.BlockSpec(memory_space=pltpu.VMEM)
    res, arrived = pl.pallas_call(
        functools.partial(fused_kernel, slices, groups, shards),
        out_shape=(
            jax.ShapeDtypeStruct((2 * rows, LANES), F32),
            jax.ShapeDtypeStruct((devices, 1, wide), I32),
        ),
        in_specs=[pl.BlockSpec(memory_space=pl.ANY), pl.BlockSpec(memory_space=pltpu.SMEM)]
        + [in_vmem] * (len(operands) - 1),
        out_specs=(pl.BlockSpec(memory_space=pl.ANY), in_vmem),
        scratch_shapes=scratch,
        compiler_params=pltpu.CompilerParams(
            collective_id=0, has_side_effects=True, vmem_limit_bytes=60 * 2**20
        ),
        cost_estimate=pl.CostEstimate(
            flops=rows * width * columns * 24, bytes_accessed=rows * width * 8,
            transcendentals=rows * columns * 4,
        ),
    )(layer_inputs_trainorder, *operands)
    out = pl.pallas_call(
        serve_kernel,
        grid=(STEPS,),
        in_specs=[
            pl.BlockSpec(memory_space=pltpu.SMEM),
            pl.BlockSpec((2 * tile, LANES), lambda i: (i, 0)),
        ],
        out_specs=pl.BlockSpec((rows, width), lambda i: (0, 0)),
        out_shape=jax.ShapeDtypeStruct((rows, width), BF16),
        scratch_shapes=[pltpu.VMEM((2 * rows, LANES), F32)],
        compiler_params=pltpu.CompilerParams(dimension_semantics=("arbitrary",)),
    )(arrived, res)
    return out[None]


def solution(mesh):
    placed = (
        P(("head", "pts"), None),
        P(("head", "pts")),
        P(),
        P(),
        P(),
        P(),
        P(),
        P(),
        P("head"),
        P(),
        P(),
        P(),
        P(),
        P(),
        P(),
        P(),
        P(),
        P(),
        P(),
        P(),
    )
    return jax.shard_map(
        body, mesh=mesh, in_specs=placed, out_specs=P("pts", "head", None), check_vma=False
    )
```

time: 175 us -> 147 us (0.84)
  Pallas kernels: 57.8 us -> 147 us
  local copies, waits for them, and re-layouts: 54.9 us -> 0 us
  starting transfers between devices: 20.2 us -> 0 us
  blocking collectives: 19.8 us -> 0 us
  other arithmetic: 14 us -> 0 us
  waiting for transfers between devices: 7.71 us -> 0 us
    pallas_call x5 -> x3, Pallas kernels: 57.8 us -> 147 us  [the longest x1 127 us: body(): pl.pallas_call(functools.partial(fused_kernel, slices, groups, shards), o...]
    gather x4 -> x0, local copies, waits for them, and re-layouts: 49.4 us -> none  [the longest x1 25.8 us: body(): return result[0][placed][None]]
    all_to_all x4 -> x0, starting transfers between devices: 20.2 us -> none  [exchange(): return lax.all_to_all(rows, both, split_axis=0, concat_axis=0, tiled=True)]
    all_to_all x2 -> x0, blocking collectives: 19.8 us -> none  [exchange(): return lax.all_to_all(rows, both, split_axis=0, concat_axis=0, tiled=True)]
    sort x2 -> x0, other arithmetic: 12.9 us -> none  [the longest x1 6.72 us: body(): _, placed = lax.sort((arrived_spots, counting), num_keys=1)]
    all_to_all x4 -> x0, waiting for transfers between devices: 7.71 us -> none  [exchange(): return lax.all_to_all(rows, both, split_axis=0, concat_axis=0, tiled=True)]
  transfers between devices with their start and end apart: 4 -> 0, of which waited for: 3 -> 0; matrix products, arithmetic and copies ran while one was open for 18% -> 0% of each run, Pallas kernels for 28% -> 0%
where the time goes in v1:
time: 147 us
  Pallas kernels  147 us (100%)
    pallas_call x1, Pallas kernels, body(): pl.pallas_call(functools.partial(fused_kernel, slices, groups, shards), o...  127 us
    pallas_call x1, Pallas kernels, body(): pl.pallas_call(serve_kernel, grid=(STEPS,), in_specs=[pl.BlockSpec(memory...  14.7 us
    pallas_call x1, Pallas kernels, body(): pl.pallas_call(functools.partial(index_kernel, groups, shards, rows), out...  4.86 us

profile of v1, /device:TPU:0, one launch (start us, length us, event | category | flops | bytes accessed | tf_op | source)
XLA Modules:
  0.0 146.8 jit_solution(379910554993007722)
XLA Ops:
  0.0 4.9 %shard_map.190 = (s32[32,256]{1,0:T(8,128)}, s32[32,1,256]{2,1,0:T(1,128)}) custom-call(s32[1,6144]{1,0:T(1,128)} %bitcast.11), custom_call_target="tpu_custom_call" | custom-call | tf_op jit(solution)/shard_map/pallas_call | solution.py:405
  4.9 127.3 %shard_map.191 = (f32[12288,128]{1,0:T(8,128)}, s32[32,1,256]{2,1,0:T(1,128)}) custom-call(bf16[6144,256]{1,0:T(8,128)(2,1)} %x_hbm.1, s32[32,256]{1,0:T(8,128)} %get-tuple-element.9.order_s, s32[32,1,256]{2,1,0:T(1,128)} %get-tuple-element.10.meta_v, f32[1,4]{1,0:T(1,128)} %bitcast.19, f32[1,256]{1,0:T(1,128)} %bitcast.13, f32[1,256]{1,0:T(1,128)} %bitcast.14, ...), custom_call_target="tpu_custom_call" | custom-call | flops 19327352832 | bytes 12582912 | tf_op jit(solution)/shard_map/pallas_call | solution.py:457
  132.2 14.7 %shard_map.192 = bf16[6144,256]{1,0:T(8,128)(2,1)} custom-call(s32[32,1,256]{2,1,0:T(1,128)} %get-tuple-element.11.spot_s, f32[12288,128]{1,0:T(8,128)} %get-tuple-element.12.res_ref), custom_call_target="tpu_custom_call" | custom-call | tf_op jit(solution)/shard_map/pallas_call | solution.py:475

commit v2 on v1

--- a/solution.py
+++ b/solution.py
@@ -11,7 +11,11 @@
 DH = 16
 LANES = 128
 STEPS = 16
-EARLY = 12
+UNITS = 32
+FIRST = 8
+EARLY = 14
+MID = 3
+AHEAD = (4, 7)
 F32 = jnp.float32
 BF16 = jnp.bfloat16
 I32 = jnp.int32
@@ -56,8 +60,19 @@
 def flip(a, b, size):
     result, bit = 0, 1
     while bit < size:
-        result = result + (a // bit + b // bit) % 2 * bit
+        result = result + lax.rem(lax.div(a, bit) + lax.div(b, bit), 2) * bit
         bit *= 2
+    return result
+
+
+def mirror(a, size):
+    result, low, high = 0, 1, size // 2
+    while high >= 1:
+        if isinstance(a, int):
+            result = result + a // low % 2 * high
+        else:
+            result = result + lax.rem(lax.div(a, low), 2) * high
+        low, high = low * 2, high // 2
     return result
 
 
@@ -68,7 +83,11 @@
     place = place_ref[...]
     block = floor_div(place, rows)
     shard = floor_div(block, groups)
-    target = (block - shard * groups) * shards + shard
+    apart = (block - shard * groups) ^ lax.axis_index("head")
+    shard = shard ^ lax.axis_index("pts")
+    bits = shards.bit_length() - 1
+    shard = sum(((shard >> at) & 1) << (bits - 1 - at) for at in range(bits))
+    target = shard * groups + apart
     target_v[...] = target
     spot_v[...] = place - block * rows
     upper = (
@@ -122,9 +141,9 @@
     slices, groups, shards,
     x_hbm, order_s, meta_v, sharp_ref, gain_ref, bias_ref, attribute_ref, feeder_ref, project_ref,
     offset_row_ref, question_ref, lookup_ref, content_ref, emit_ref, emit_bias_ref,
-    gain2_ref, bias2_ref, entry_ref, entry_bias_ref, exit_ref, exit_bias_ref,
+    gain2_ref, bias2_ref, entry_bias_ref, exit_bias_ref, entry_hbm, exit_hbm,
     res_hbm, meta_in,
-    x_v, xf, stage, send_v, recv_v, res,
+    x_v, xf, stage, send_v, recv_v, res, share_v, entry_ref, exit_ref,
     sharp_v, sharp_in, w_ref, expand_ref, offset_ref, scale_ref, numer, total,
     part_out, part_in, mine, all_in, sums_v, blend,
     local_sem, out_sem, row_send, row_recv, meta_send, meta_recv, sharp_send, sharp_recv,
@@ -140,12 +159,20 @@
     my_head, my_pts = lax.axis_index("head"), lax.axis_index("pts")
     me = my_head * shards + my_pts
 
+    unit = devices // UNITS
+    heads = [flip(my_head, jnp.int32(at), groups) for at in range(groups)]
+    shard_ids = [flip(my_pts, jnp.int32(at), shards) for at in range(shards)]
+
     def peer(slot):
-        return flip(my_head, slot % groups, groups), flip(my_pts, slot // groups, shards)
+        return heads[slot % groups], shard_ids[mirror(slot // groups, shards)]
 
     def flat(slot):
         head, pts = peer(slot)
         return head * shards + pts
+
+    def each_peer(step):
+        for slot in range(1, devices):
+            step(slot)
 
     def loop(low, high, step):
         def run(at, carry):
@@ -154,11 +181,15 @@
         lax.fori_loop(low, high, run, 0)
 
     barrier = pltpu.get_barrier_semaphore()
-    loop(1, devices, lambda slot: pl.semaphore_signal(
+    load = pltpu.make_async_copy(x_hbm, x_v, local_sem.at[0])
+    load.start()
+    each_peer(lambda slot: pl.semaphore_signal(
         barrier, 1, device_id=peer(slot), device_id_type=MESH
     ))
-    load = pltpu.make_async_copy(x_hbm, x_v, local_sem.at[0])
-    load.start()
+    entry_load = pltpu.make_async_copy(entry_hbm, entry_ref, local_sem.at[1])
+    exit_load = pltpu.make_async_copy(exit_hbm, exit_ref, local_sem.at[2])
+    entry_load.start()
+    exit_load.start()
 
     sharp_v[...] = jnp.zeros_like(sharp_v)
     sharp_v[:, :own] = sharp_ref[...]
@@ -177,26 +208,52 @@
     numer[...] = jnp.zeros_like(numer)
     total[...] = jnp.zeros_like(total)
 
+    load.wait()
+
+    def widen(at):
+        part = x_v[pl.ds(pl.multiple_of(at * tile, tile), tile), :].astype(F32)
+        xf[pl.ds(at * 2 * tile, tile, stride=2), :] = part[:, :LANES]
+        xf[pl.ds(at * 2 * tile + 1, tile, stride=2), :] = part[:, LANES:]
+
+    def collect(at):
+        for k in range(tile):
+            stage[2 * k : 2 * k + 2, :] = xf[
+                pl.ds(order_s[at * blocks + k // per_pair, k % per_pair] * 2, 2), :
+            ]
+        span = pl.ds(pl.multiple_of(at * tile, tile), tile)
+        send_v[span, :LANES] = stage[pl.ds(0, tile, stride=2), :].astype(BF16)
+        send_v[span, LANES:] = stage[pl.ds(1, tile, stride=2), :].astype(BF16)
+
+    loop(0, STEPS, widen)
+    loop(0, STEPS // 2, collect)
     pl.semaphore_wait(barrier, devices - 1)
 
     def sharp_copy(step):
         return pltpu.make_async_remote_copy(
             sharp_v, sharp_in.at[my_head], sharp_send.at[step], sharp_recv.at[step],
-            device_id=(flip(my_head, step, groups), my_pts), device_id_type=MESH,
+            device_id=(heads[step], my_pts), device_id_type=MESH,
         )
 
     def meta_copy(slot):
         return pltpu.make_async_remote_copy(
-            meta_v.at[flat(slot)], meta_in.at[slot], meta_send.at[slot], meta_recv.at[slot],
+            meta_v.at[slot], meta_in.at[slot], meta_send.at[slot], meta_recv.at[slot],
             device_id=peer(slot), device_id_type=MESH,
         )
 
-    def row_copy(slot):
+    def row_copy(slot, goal):
         span = pl.ds(pl.multiple_of(slot * per_pair, per_pair), per_pair)
         return pltpu.make_async_remote_copy(
             send_v.at[span], recv_v.at[span], row_send.at[slot], row_recv.at[slot],
-            device_id=peer(slot), device_id_type=MESH,
-        )
+            device_id=goal, device_id_type=MESH,
+        )
+
+    def far_goal(slot):
+        shard = mirror(lax.div(slot, groups), shards)
+        return flip(my_head, lax.rem(slot, groups), groups), flip(my_pts, shard, shards)
+
+    def send_units(low, high):
+        for slot in range(max(low * unit, 1), high * unit):
+            row_copy(slot, peer(slot)).start()
 
     def part_copy(slot):
         return pltpu.make_async_remote_copy(
@@ -210,19 +267,12 @@
             device_id=peer(slot), device_id_type=MESH,
         )
 
-    loop(1, groups, lambda step: sharp_copy(step).start())
-    loop(1, devices, lambda slot: meta_copy(slot).start())
-    meta_in[0] = meta_v[me]
-
-    load.wait()
-
-    def widen(at):
-        part = x_v[pl.ds(pl.multiple_of(at * tile, tile), tile), :].astype(F32)
-        xf[pl.ds(at * 2 * tile, tile, stride=2), :] = part[:, :LANES]
-        xf[pl.ds(at * 2 * tile + 1, tile, stride=2), :] = part[:, LANES:]
-
-    loop(0, STEPS, widen)
-    loop(1, groups, lambda step: sharp_copy(step).wait())
+    for step in range(1, groups):
+        sharp_copy(step).start()
+    send_units(0, FIRST)
+    loop(STEPS // 2, STEPS, collect)
+    for step in range(1, groups):
+        sharp_copy(step).wait()
     per_group = own * slices
     for group in range(groups):
         lane = lax.broadcasted_iota(I32, (per_group, LANES), 1)
@@ -231,24 +281,14 @@
         scale_ref[group * per_group : (group + 1) * per_group] = LOG2E / sharp
 
     def sums_step(at):
-        @pl.when(jnp.logical_and(at > 0, at <= EARLY // blocks))
+        @pl.when(lax.rem(at * (EARLY - FIRST), STEPS) < EARLY - FIRST)
         def _():
-            for way in range(blocks):
-                slot = (at - 1) * blocks + way
-
-                @pl.when(slot > 0)
-                def _():
-                    row_copy(slot).start()
-
-        for way in range(blocks):
-            goal = flat(at * blocks + way)
-            for k in range(per_pair):
-                put = 2 * (way * per_pair + k)
-                stage[put : put + 2, :] = xf[pl.ds(order_s[goal, k] * 2, 2), :]
+            at_unit = FIRST + lax.div(at * (EARLY - FIRST), STEPS)
+            for way in range(unit):
+                slot = at_unit * unit + way
+                row_copy(slot, far_goal(slot)).start()
+
         span = pl.ds(pl.multiple_of(at * tile, tile), tile)
-        send_v[span, :LANES] = stage[pl.ds(0, tile, stride=2), :].astype(BF16)
-        send_v[span, LANES:] = stage[pl.ds(1, tile, stride=2), :].astype(BF16)
-
         normed = norm_rows(x_v[span, :].astype(F32), gain_ref[...], bias_ref[...])
         both = lax.dot_general(w_ref[...], normed, NT, preferred_element_type=F32).astype(BF16)
         share = slice_weights(
@@ -278,15 +318,43 @@
     part_out[...] = jnp.zeros_like(part_out)
     for line, low, piece, inner in places:
         part_out[piece, inner : inner + 1, :] = sums_v[line : line + 1, low : low + LANES]
-    loop(1, devices, lambda slot: part_copy(slot).start())
+    each_peer(lambda slot: part_copy(slot).start())
     part_in[0] = part_out[me]
-    loop(max(EARLY, 1), devices, lambda slot: row_copy(slot).start())
-
-    loop(1, devices, lambda slot: part_copy(slot).wait())
+    send_units(EARLY, EARLY + MID)
+    each_peer(lambda slot: meta_copy(slot).start())
+    meta_in[0] = meta_v[0]
+    recv_v[:per_pair] = send_v[:per_pair]
+
+    def wait_rows(at):
+        for way in range(blocks):
+            slot = at * blocks + way
+
+            @pl.when(slot > 0)
+            def _():
+                row_copy(slot, (my_head, my_pts)).wait_recv()
+
+    def weigh(at):
+        x = recv_v[pl.ds(pl.multiple_of(at * tile, tile), tile), :].astype(F32)
+        normed = norm_rows(x, gain_ref[...], bias_ref[...])
+        feeder = lax.dot_general(
+            w_ref[width:], normed, NT, preferred_element_type=F32
+        ).astype(BF16)
+        share = slice_weights(feeder, expand_ref[...], offset_ref[...], scale_ref[...], slices)
+        return share.astype(BF16)
+
+    def weigh_ahead(at):
+        wait_rows(at)
+        share_v[at] = weigh(at)
+
+    loop(0, AHEAD[0], weigh_ahead)
+
+    each_peer(lambda slot: part_copy(slot).wait())
     mine[...] = jnp.sum(part_in[...], axis=0)
-    loop(1, devices, lambda slot: all_copy(slot).start())
+    each_peer(lambda slot: all_copy(slot).start())
+    send_units(EARLY + MID, UNITS)
     all_in[me] = mine[...]
-    loop(1, devices, lambda slot: all_copy(slot).wait())
+    loop(AHEAD[0], AHEAD[1], weigh_ahead)
+    each_peer(lambda slot: all_copy(slot).wait())
     for line, low, piece, inner in places:
         sums_v[line : line + 1, low : low + LANES] = all_in[piece, inner : inner + 1, :]
 
@@ -304,24 +372,12 @@
     sout = jnp.dot(value, attention, precision=HIGHEST, preferred_element_type=F32)
     spread = jnp.concatenate([sout] * (width // DH), axis=0)
     blend[...] = jnp.where(same_head(blend.shape, DH, slices), spread, 0.0).astype(BF16)
-    recv_v[:per_pair] = send_v[:per_pair]
-
-    def rows_step(at):
-        def arrived(way):
-            slot = at * blocks + way
-
-            @pl.when(slot > 0)
-            def _():
-                row_copy(slot).wait_recv()
-
-        loop(0, blocks, arrived)
+    entry_load.wait()
+    exit_load.wait()
+
+    def finish(at, share):
         x = recv_v[pl.ds(pl.multiple_of(at * tile, tile), tile), :].astype(F32)
-        normed = norm_rows(x, gain_ref[...], bias_ref[...])
-        feeder = lax.dot_general(
-            w_ref[width:], normed, NT, preferred_element_type=F32
-        ).astype(BF16)
-        share = slice_weights(feeder, expand_ref[...], offset_ref[...], scale_ref[...], slices)
-        mixed = jnp.dot(blend[...], share.astype(BF16), preferred_element_type=F32)
+        mixed = jnp.dot(blend[...], share, preferred_element_type=F32)
         y = (
             x
             + jnp.dot(mixed.T.astype(BF16), emit_ref[...], preferred_element_type=F32)
@@ -341,33 +397,57 @@
         span = pl.ds(pl.multiple_of(at * 2 * tile, 2 * tile), 2 * tile)
         return pltpu.make_async_copy(res.at[span], res_hbm.at[span], out_sem.at[at])
 
-    loop(0, STEPS, rows_step)
-    loop(1, devices, lambda slot: meta_copy(slot).wait())
-    loop(1, devices, lambda slot: row_copy(slot).wait_send())
+    loop(0, AHEAD[1], lambda at: finish(at, share_v[at]))
+
+    def rows_step(at):
+        wait_rows(at)
+        finish(at, weigh(at))
+
+    loop(AHEAD[1], STEPS, rows_step)
+    each_peer(lambda slot: meta_copy(slot).wait())
+    each_peer(lambda slot: row_copy(slot, peer(slot)).wait_send())
     loop(0, STEPS, lambda at: out_copy(at).wait())
 
 
-def serve_kernel(spot_s, res_ref, out_ref, placed):
-    step = pl.program_id(0)
-    tile = res_ref.shape[0] // 2
-    blocks = spot_s.shape[0] // pl.num_programs(0)
+def serve_kernel(spot_s, res_hbm, out_hbm, res, placed, out_v, in_sem, out_sem):
+    rows = out_v.shape[0]
+    tile = rows // STEPS
+    blocks = spot_s.shape[0] // STEPS
     per_pair = tile // blocks
-    for way in range(blocks):
-        for k in range(per_pair):
-            spot = spot_s[step * blocks + way, 0, k]
-            at = 2 * (way * per_pair + k)
-            placed[pl.ds(pl.multiple_of(spot * 2, 2), 2), :] = res_ref[at : at + 2, :]
-
-    @pl.when(step == pl.num_programs(0) - 1)
-    def _():
-        def narrow(at, carry):
-            span = pl.ds(pl.multiple_of(at * tile, tile), tile)
-            out_ref[span, :LANES] = placed[pl.ds(at * 2 * tile, tile, stride=2), :].astype(BF16)
-            out_ref[span, LANES:] = placed[pl.ds(at * 2 * tile + 1, tile, stride=2), :].astype(
-                BF16
-            )
-            return carry
-        lax.fori_loop(0, out_ref.shape[0] // tile, narrow, 0)
+
+    def res_copy(at):
+        span = pl.ds(pl.multiple_of(at * 2 * tile, 2 * tile), 2 * tile)
+        return pltpu.make_async_copy(res_hbm.at[span], res.at[span], in_sem.at[at])
+
+    def out_copy(at):
+        span = pl.ds(pl.multiple_of(at * tile, tile), tile)
+        return pltpu.make_async_copy(out_v.at[span], out_hbm.at[span], out_sem.at[at])
+
+    for at in range(STEPS):
+        res_copy(at).start()
+
+    def scatter(at, carry):
+        res_copy(at).wait()
+        for way in range(blocks):
+            slot = at * blocks + way
+            for k in range(per_pair):
+                spot = pl.multiple_of(spot_s[slot, 0, k] * 2, 2)
+                row = pl.multiple_of(at * 2 * tile, 2 * tile) + 2 * (way * per_pair + k)
+                placed[pl.ds(spot, 2), :] = res[pl.ds(pl.multiple_of(row, 2), 2), :]
+        return carry
+
+    lax.fori_loop(0, STEPS, scatter, 0)
+
+    def narrow(at, carry):
+        span = pl.ds(pl.multiple_of(at * tile, tile), tile)
+        out_v[span, :LANES] = placed[pl.ds(at * 2 * tile, tile, stride=2), :].astype(BF16)
+        out_v[span, LANES:] = placed[pl.ds(at * 2 * tile + 1, tile, stride=2), :].astype(BF16)
+        out_copy(at).start()
+        return carry
+
+    lax.fori_loop(0, STEPS, narrow, 0)
+    for at in range(STEPS):
+        out_copy(at).wait()
 
 
 def body(
@@ -415,8 +495,9 @@
         initial_layernorm_offset[None], attribute_projection, assignment_feeder_projection,
         partition_projection, partition_offset[None], partition_question_map,
         partition_lookup_map, partition_content_map, emitted_projection, emitted_offset[None],
-        latter_layernorm_gain[None], latter_layernorm_offset[None], perceptron_entry_map,
-        perceptron_entry_offset[None], perceptron_exit_map, perceptron_exit_offset[None],
+        latter_layernorm_gain[None], latter_layernorm_offset[None],
+        perceptron_entry_offset[None], perceptron_exit_offset[None], perceptron_entry_map,
+        perceptron_exit_map,
     )
     dma = pltpu.SemaphoreType.DMA
     scratch = [
@@ -426,6 +507,9 @@
         pltpu.VMEM((rows, width), BF16),
         pltpu.VMEM((rows, width), BF16),
         pltpu.VMEM((2 * rows, LANES), F32),
+        pltpu.VMEM((AHEAD[1], columns, tile), BF16),
+        pltpu.VMEM(perceptron_entry_map.shape, BF16),
+        pltpu.VMEM(perceptron_exit_map.shape, BF16),
         pltpu.VMEM((1, LANES), F32),
         pltpu.VMEM((groups, 1, LANES), F32),
         pltpu.VMEM((2 * width, width), BF16),
@@ -440,7 +524,7 @@
         pltpu.VMEM((devices, depth, LANES), F32),
         pltpu.VMEM((DH + 8, columns), F32),
         pltpu.VMEM((width, columns), BF16),
-        dma((2,)),
+        dma((3,)),
         dma((STEPS,)),
         dma((devices,)),
         dma((devices,)),
@@ -461,7 +545,8 @@
             jax.ShapeDtypeStruct((devices, 1, wide), I32),
         ),
         in_specs=[pl.BlockSpec(memory_space=pl.ANY), pl.BlockSpec(memory_space=pltpu.SMEM)]
-        + [in_vmem] * (len(operands) - 1),
+        + [in_vmem] * (len(operands) - 3)
+        + [pl.BlockSpec(memory_space=pl.ANY)] * 2,
         out_specs=(pl.BlockSpec(memory_space=pl.ANY), in_vmem),
         scratch_shapes=scratch,
         compiler_params=pltpu.CompilerParams(
@@ -472,17 +557,19 @@
             transcendentals=rows * columns * 4,
         ),
     )(layer_inputs_trainorder, *operands)
+    anywhere = pl.BlockSpec(memory_space=pl.ANY)
     out = pl.pallas_call(
         serve_kernel,
-        grid=(STEPS,),
-        in_specs=[
-            pl.BlockSpec(memory_space=pltpu.SMEM),
-            pl.BlockSpec((2 * tile, LANES), lambda i: (i, 0)),
+        in_specs=[pl.BlockSpec(memory_space=pltpu.SMEM), anywhere],
+        out_specs=anywhere,
+        out_shape=jax.ShapeDtypeStruct((rows, width), BF16),
+        scratch_shapes=[
+            pltpu.VMEM((2 * rows, LANES), F32),
+            pltpu.VMEM((2 * rows, LANES), F32),
+            pltpu.VMEM((rows, width), BF16),
+            dma((STEPS,)),
+            dma((STEPS,)),
         ],
-        out_specs=pl.BlockSpec((rows, width), lambda i: (0, 0)),
-        out_shape=jax.ShapeDtypeStruct((rows, width), BF16),
-        scratch_shapes=[pltpu.VMEM((2 * rows, LANES), F32)],
-        compiler_params=pltpu.CompilerParams(dimension_semantics=("arbitrary",)),
     )(arrived, res)
     return out[None]
 

time: 147 us -> 105 us (0.71)
  Pallas kernels: 147 us -> 104 us
    pallas_call x1, Pallas kernels: 127 us -> 88 us  [body(): pl.pallas_call(functools.partial(fused_kernel, slices, groups, shards), o...]
    pallas_call x1, Pallas kernels: 14.7 us -> 10.7 us  [body(): pl.pallas_call(serve_kernel, in_specs=[pl.BlockSpec(memory_space=pltpu.SM...]
where the time goes in v2:
time: 105 us; the launch traced here: 104 us
  Pallas kernels  104 us (99%)
    pallas_call x1, Pallas kernels, body(): pl.pallas_call(functools.partial(fused_kernel, slices, groups, shards), o...  88 us
    pallas_call x1, Pallas kernels, body(): pl.pallas_call(serve_kernel, in_specs=[pl.BlockSpec(memory_space=pltpu.SM...  10.7 us
    pallas_call x1, Pallas kernels, body(): pl.pallas_call(functools.partial(index_kernel, groups, shards, rows), out...  4.87 us

profile of v2, /device:TPU:0, one launch (start us, length us, event | category | flops | bytes accessed | tf_op | source)
XLA Modules:
  0.0 103.6 jit_solution(15203609594592628366)
XLA Ops:
  0.0 4.9 %shard_map.190 = (s32[32,256]{1,0:T(8,128)}, s32[32,1,256]{2,1,0:T(1,128)}) custom-call(s32[1,6144]{1,0:T(1,128)} %bitcast.11), custom_call_target="tpu_custom_call" | custom-call | tf_op jit(solution)/shard_map/pallas_call | solution.py:485
  4.9 88.0 %shard_map.191 = (f32[12288,128]{1,0:T(8,128)}, s32[32,1,256]{2,1,0:T(1,128)}) custom-call(bf16[6144,256]{1,0:T(8,128)(2,1)} %x_hbm.1, s32[32,256]{1,0:T(8,128)} %get-tuple-element.9.order_s, s32[32,1,256]{2,1,0:T(1,128)} %get-tuple-element.10.meta_v, f32[1,4]{1,0:T(1,128)} %bitcast.19, f32[1,256]{1,0:T(1,128)} %bitcast.13, f32[1,256]{1,0:T(1,128)} %bitcast.14, ...), custom_call_target="tpu_custom_call" | custom-call | flops 19327352832 | bytes 12582912 | tf_op jit(solution)/shard_map/pallas_call | solution.py:541
  92.9 10.7 %shard_map.192 = bf16[6144,256]{1,0:T(8,128)(2,1)} custom-call(s32[32,1,256]{2,1,0:T(1,128)} %get-tuple-element.11.spot_s, f32[12288,128]{1,0:T(8,128)} %get-tuple-element.12.res_hbm), custom_call_target="tpu_custom_call" | custom-call | tf_op jit(solution)/shard_map/pallas_call | solution.py:561

commit v3 on v2

--- a/solution.py
+++ b/solution.py
@@ -11,9 +11,11 @@
 DH = 16
 LANES = 128
 STEPS = 16
+SUM_STEPS = 12
+PARTS = 4
 UNITS = 32
 FIRST = 8
-EARLY = 14
+EARLY = 12
 MID = 3
 AHEAD = (4, 7)
 F32 = jnp.float32
@@ -109,8 +111,8 @@
         rank_v[:, at * LANES : (at + 1) * LANES] = ahead.astype(I32)
         run = run + prefix[span][:, LANES - 1 :]
 
-    wide = order_ref.shape[1]
-    part_lanes = 4 * LANES
+    per_pair = order_ref.shape[1]
+    part_lanes = 8 * LANES
 
     def invert(at, total_so_far):
         lanes = pl.ds(pl.multiple_of(at * part_lanes, part_lanes), part_lanes)
@@ -118,7 +120,7 @@
             lax.broadcasted_iota(I32, (devices, part_lanes), 0) == target_v[:, lanes]
         ).astype(F32)
         slot_hot = (
-            lax.broadcasted_iota(I32, (wide, part_lanes), 0) == rank_v[:, lanes]
+            lax.broadcasted_iota(I32, (per_pair, part_lanes), 0) == rank_v[:, lanes]
         ).astype(F32).astype(BF16)
         index = lax.broadcasted_iota(I32, (1, part_lanes), 1) + at * part_lanes
         values = []
@@ -129,12 +131,13 @@
         return total_so_far + lax.dot_general(values, slot_hot, NT, preferred_element_type=F32)
 
     table = lax.fori_loop(
-        0, rows // part_lanes, invert, jnp.zeros((4 * devices, wide), F32)
+        0, rows // part_lanes, invert, jnp.zeros((4 * devices, per_pair), F32)
     )
-    order_ref[...] = (table[:devices] * 64.0 + table[devices : 2 * devices]).astype(I32)
-    spots = table[2 * devices : 3 * devices] * 64.0 + table[3 * devices :]
+    order_ref[...] = (table[:devices] * 128.0 + table[devices : 2 * devices] * 2.0).astype(I32)
+    spots = table[2 * devices : 3 * devices] * 128.0 + table[3 * devices :] * 2.0
+    spots_ref[...] = jnp.zeros_like(spots_ref)
     for at in range(devices):
-        spots_ref[at] = spots[at : at + 1].astype(I32)
+        spots_ref[at, :, :per_pair] = spots[at : at + 1].astype(I32)
 
 
 def fused_kernel(
@@ -154,6 +157,7 @@
     per_pair = rows // devices
     tile = rows // STEPS
     blocks = devices // STEPS
+    sum_tile = rows // SUM_STEPS
     columns = expand_ref.shape[0]
     own = sharp_ref.shape[1]
     my_head, my_pts = lax.axis_index("head"), lax.axis_index("pts")
@@ -216,16 +220,19 @@
         xf[pl.ds(at * 2 * tile + 1, tile, stride=2), :] = part[:, LANES:]
 
     def collect(at):
-        for k in range(tile):
-            stage[2 * k : 2 * k + 2, :] = xf[
-                pl.ds(order_s[at * blocks + k // per_pair, k % per_pair] * 2, 2), :
-            ]
-        span = pl.ds(pl.multiple_of(at * tile, tile), tile)
+        for way in range(blocks):
+            def take(k, carry):
+                put = pl.multiple_of(2 * (way * per_pair + k), 2)
+                stage[pl.ds(put, 2), :] = xf[pl.ds(order_s[at * blocks + way, k], 2), :]
+                return carry
+            lax.fori_loop(0, per_pair, take, 0, unroll=True)
+        span = slice(at * tile, (at + 1) * tile)
         send_v[span, :LANES] = stage[pl.ds(0, tile, stride=2), :].astype(BF16)
         send_v[span, LANES:] = stage[pl.ds(1, tile, stride=2), :].astype(BF16)
 
     loop(0, STEPS, widen)
-    loop(0, STEPS // 2, collect)
+    for at in range(STEPS // 2):
+        collect(at)
     pl.semaphore_wait(barrier, devices - 1)
 
     def sharp_copy(step):
@@ -270,7 +277,8 @@
     for step in range(1, groups):
         sharp_copy(step).start()
     send_units(0, FIRST)
-    loop(STEPS // 2, STEPS, collect)
+    for at in range(STEPS // 2, STEPS):
+        collect(at)
     for step in range(1, groups):
         sharp_copy(step).wait()
     per_group = own * slices
@@ -281,14 +289,14 @@
         scale_ref[group * per_group : (group + 1) * per_group] = LOG2E / sharp
 
     def sums_step(at):
-        @pl.when(lax.rem(at * (EARLY - FIRST), STEPS) < EARLY - FIRST)
+        @pl.when(lax.rem(at * (EARLY - FIRST), SUM_STEPS) < EARLY - FIRST)
         def _():
-            at_unit = FIRST + lax.div(at * (EARLY - FIRST), STEPS)
+            at_unit = FIRST + lax.div(at * (EARLY - FIRST), SUM_STEPS)
             for way in range(unit):
                 slot = at_unit * unit + way
                 row_copy(slot, far_goal(slot)).start()
 
-        span = pl.ds(pl.multiple_of(at * tile, tile), tile)
+        span = pl.ds(pl.multiple_of(at * sum_tile, sum_tile), sum_tile)
         normed = norm_rows(x_v[span, :].astype(F32), gain_ref[...], bias_ref[...])
         both = lax.dot_general(w_ref[...], normed, NT, preferred_element_type=F32).astype(BF16)
         share = slice_weights(
@@ -298,11 +306,11 @@
             both[:width], share.astype(BF16), NT, preferred_element_type=F32
         )
         part = share[:, :LANES]
-        for low in range(LANES, tile, LANES):
+        for low in range(LANES, sum_tile, LANES):
             part += share[:, low : low + LANES]
         total[...] += part
 
-    loop(0, STEPS, sums_step)
+    loop(0, SUM_STEPS, sums_step)
 
     kept = jnp.where(same_head(numer.shape, DH, slices), numer[...], 0.0)
     sums_v[:DH] = jnp.sum(kept.reshape(-1, DH, columns), axis=0)
@@ -412,6 +420,7 @@
 def serve_kernel(spot_s, res_hbm, out_hbm, res, placed, out_v, in_sem, out_sem):
     rows = out_v.shape[0]
     tile = rows // STEPS
+    part = rows // PARTS
     blocks = spot_s.shape[0] // STEPS
     per_pair = tile // blocks
 
@@ -420,33 +429,32 @@
         return pltpu.make_async_copy(res_hbm.at[span], res.at[span], in_sem.at[at])
 
     def out_copy(at):
-        span = pl.ds(pl.multiple_of(at * tile, tile), tile)
+        span = pl.ds(pl.multiple_of(at * part, part), part)
         return pltpu.make_async_copy(out_v.at[span], out_hbm.at[span], out_sem.at[at])
 
     for at in range(STEPS):
         res_copy(at).start()
 
-    def scatter(at, carry):
+    for at in range(STEPS):
         res_copy(at).wait()
-        for way in range(blocks):
-            slot = at * blocks + way
-            for k in range(per_pair):
-                spot = pl.multiple_of(spot_s[slot, 0, k] * 2, 2)
-                row = pl.multiple_of(at * 2 * tile, 2 * tile) + 2 * (way * per_pair + k)
-                placed[pl.ds(spot, 2), :] = res[pl.ds(pl.multiple_of(row, 2), 2), :]
-        return carry
-
-    lax.fori_loop(0, STEPS, scatter, 0)
+        for slot in range(at * blocks, (at + 1) * blocks):
+            def put(k, carry):
+                spot = pl.multiple_of(spot_s[slot, 0, k], 2)
+                low = pl.multiple_of(2 * (slot * per_pair + k), 2)
+                placed[pl.ds(spot, 2), :] = res[pl.ds(low, 2), :]
+                return carry
+            lax.fori_loop(0, per_pair, put, 0, unroll=True)
 
     def narrow(at, carry):
-        span = pl.ds(pl.multiple_of(at * tile, tile), tile)
-        out_v[span, :LANES] = placed[pl.ds(at * 2 * tile, tile, stride=2), :].astype(BF16)
-        out_v[span, LANES:] = placed[pl.ds(at * 2 * tile + 1, tile, stride=2), :].astype(BF16)
+        first = at * 2 * part
+        span = pl.ds(pl.multiple_of(at * part, part), part)
+        out_v[span, :LANES] = placed[pl.ds(first, part, stride=2), :].astype(BF16)
+        out_v[span, LANES:] = placed[pl.ds(first + 1, part, stride=2), :].astype(BF16)
         out_copy(at).start()
         return carry
 
-    lax.fori_loop(0, STEPS, narrow, 0)
-    for at in range(STEPS):
+    lax.fori_loop(0, PARTS, narrow, 0)
+    for at in range(PARTS):
         out_copy(at).wait()
 
 
@@ -485,7 +493,7 @@
     order, spots = pl.pallas_call(
         functools.partial(index_kernel, groups, shards, rows),
         out_shape=(
-            jax.ShapeDtypeStruct((devices, wide), I32),
+            jax.ShapeDtypeStruct((devices, per_pair), I32),
             jax.ShapeDtypeStruct((devices, 1, wide), I32),
         ),
         scratch_shapes=[pltpu.VMEM((1, rows), I32)] * 3,
@@ -568,7 +576,7 @@
             pltpu.VMEM((2 * rows, LANES), F32),
             pltpu.VMEM((rows, width), BF16),
             dma((STEPS,)),
-            dma((STEPS,)),
+            dma((PARTS,)),
         ],
     )(arrived, res)
     return out[None]

time: 105 us -> 99 us (0.943)
  Pallas kernels: 104 us -> 97.6 us
    pallas_call x1, Pallas kernels: 10.7 us -> 7.47 us  [body(): pl.pallas_call(serve_kernel, in_specs=[pl.BlockSpec(memory_space=pltpu.SM...]
    pallas_call x1, Pallas kernels: 88 us -> 86.5 us  [body(): pl.pallas_call(functools.partial(fused_kernel, slices, groups, shards), o...]
    pallas_call x1, Pallas kernels: 4.87 us -> 3.67 us  [body(): pl.pallas_call(functools.partial(index_kernel, groups, shards, rows), out...]
where the time goes in v3:
time: 99 us; the launch traced here: 97.8 us
  Pallas kernels  97.6 us (99%)
    pallas_call x1, Pallas kernels, body(): pl.pallas_call(functools.partial(fused_kernel, slices, groups, shards), o...  86.5 us
    pallas_call x1, Pallas kernels, body(): pl.pallas_call(serve_kernel, in_specs=[pl.BlockSpec(memory_space=pltpu.SM...  7.47 us
    pallas_call x1, Pallas kernels, body(): pl.pallas_call(functools.partial(index_kernel, groups, shards, rows), out...  3.67 us

profile of v3, /device:TPU:0, one launch (start us, length us, event | category | flops | bytes accessed | tf_op | source)
XLA Modules:
  0.0 97.8 jit_solution(16414986525851260033)
XLA Ops:
  0.0 3.7 %shard_map.190 = (s32[32,192]{1,0:T(8,128)}, s32[32,1,256]{2,1,0:T(1,128)}) custom-call(s32[1,6144]{1,0:T(1,128)} %bitcast.11), custom_call_target="tpu_custom_call" | custom-call | tf_op jit(solution)/shard_map/pallas_call | solution.py:493
  3.7 86.5 %shard_map.191 = (f32[12288,128]{1,0:T(8,128)}, s32[32,1,256]{2,1,0:T(1,128)}) custom-call(bf16[6144,256]{1,0:T(8,128)(2,1)} %x_hbm.1, s32[32,192]{1,0:T(8,128)} %get-tuple-element.9.order_s, s32[32,1,256]{2,1,0:T(1,128)} %get-tuple-element.10.meta_v, f32[1,4]{1,0:T(1,128)} %bitcast.19, f32[1,256]{1,0:T(1,128)} %bitcast.13, f32[1,256]{1,0:T(1,128)} %bitcast.14, ...), custom_call_target="tpu_custom_call" | custom-call | flops 19327352832 | bytes 12582912 | tf_op jit(solution)/shard_map/pallas_call | solution.py:549
  90.2 7.5 %shard_map.192 = bf16[6144,256]{1,0:T(8,128)(2,1)} custom-call(s32[32,1,256]{2,1,0:T(1,128)} %get-tuple-element.11.spot_s, f32[12288,128]{1,0:T(8,128)} %get-tuple-element.12.res_hbm), custom_call_target="tpu_custom_call" | custom-call | tf_op jit(solution)/shard_map/pallas_call | solution.py:569

commit v4 on v3

--- a/solution.py
+++ b/solution.py
@@ -15,9 +15,9 @@
 PARTS = 4
 UNITS = 32
 FIRST = 8
-EARLY = 12
-MID = 3
-AHEAD = (4, 7)
+EARLY = 11
+MID = 1
+AHEAD = (3, 8)
 F32 = jnp.float32
 BF16 = jnp.bfloat16
 I32 = jnp.int32

time: 99 us -> 98.7 us (level)
  no operation moved by 1% of the time
where the time goes in v4:
time: 98.7 us; the launch traced here: 97.8 us
  Pallas kernels  97.6 us (99%)
    pallas_call x1, Pallas kernels, body(): pl.pallas_call(functools.partial(fused_kernel, slices, groups, shards), o...  86.4 us
    pallas_call x1, Pallas kernels, body(): pl.pallas_call(serve_kernel, in_specs=[pl.BlockSpec(memory_space=pltpu.SM...  7.47 us
    pallas_call x1, Pallas kernels, body(): pl.pallas_call(functools.partial(index_kernel, groups, shards, rows), out...  3.67 us

profile of v4, /device:TPU:0, one launch (start us, length us, event | category | flops | bytes accessed | tf_op | source)
XLA Modules:
  0.0 97.8 jit_solution(6758186291658014885)
XLA Ops:
  0.0 3.7 %shard_map.190 = (s32[32,192]{1,0:T(8,128)}, s32[32,1,256]{2,1,0:T(1,128)}) custom-call(s32[1,6144]{1,0:T(1,128)} %bitcast.11), custom_call_target="tpu_custom_call" | custom-call | tf_op jit(solution)/shard_map/pallas_call | solution.py:493
  3.7 86.4 %shard_map.191 = (f32[12288,128]{1,0:T(8,128)}, s32[32,1,256]{2,1,0:T(1,128)}) custom-call(bf16[6144,256]{1,0:T(8,128)(2,1)} %x_hbm.1, s32[32,192]{1,0:T(8,128)} %get-tuple-element.9.order_s, s32[32,1,256]{2,1,0:T(1,128)} %get-tuple-element.10.meta_v, f32[1,4]{1,0:T(1,128)} %bitcast.19, f32[1,256]{1,0:T(1,128)} %bitcast.13, f32[1,256]{1,0:T(1,128)} %bitcast.14, ...), custom_call_target="tpu_custom_call" | custom-call | flops 19327352832 | bytes 12582912 | tf_op jit(solution)/shard_map/pallas_call | solution.py:549
  90.1 7.5 %shard_map.192 = bf16[6144,256]{1,0:T(8,128)(2,1)} custom-call(s32[32,1,256]{2,1,0:T(1,128)} %get-tuple-element.11.spot_s, f32[12288,128]{1,0:T(8,128)} %get-tuple-element.12.res_hbm), custom_call_target="tpu_custom_call" | custom-call | tf_op jit(solution)/shard_map/pallas_call | solution.py:569
